TPU v7x, 128 devices: a whole 4x4x4 slice. The times are simulated.
128 devices in a mesh: gx: 8 (over z_hi, x), gy: 4 (over z_lo, core), gz: 4 (over y).
Axes of the slice: x: 4, y: 4, z: 4 (z_hi: 2, z_lo: 2; z = z_hi * 2 + z_lo), core: 2. Of those that a mesh axis runs over, the one named last changes fastest.
Arguments:
- calcium: float32 [8, 256, 128, 512], P(None, 'gx', 'gz', 'gy'), may hold values from 0.1 to 3
- activation: float32 [8, 256, 128, 512], P(None, 'gx', 'gz', 'gy'), may hold values from 0 to 1
- element_first: int32 [256], replicated, may hold values from 0 to 63, as said below
- offset_first: float32 [256], replicated, may hold values from 0.1 to 0.9
- element_second: int32 [512], replicated, may hold values from 0 to 127, as said below
- offset_second: float32 [512], replicated, may hold values from 0.1 to 0.9
- element_third: int32 [128], replicated, may hold values from 0 to 31, as said below
- offset_third: float32 [128], replicated, may hold values from 0.1 to 0.9
- troponin: float32 [64, 32, 128], P('gx', ('gy', 'gz')), may hold values from 0 to 1
- tension: float32 [64, 32, 128], P('gx', ('gy', 'gz')), may hold values from 0 to 2
- unbind_rate: float32 [64, 32, 128], P('gx', ('gy', 'gz')), may hold values from 0.2 to 2
- relax_rate: float32 [64, 32, 128], P('gx', ('gy', 'gz')), may hold values from 0.5 to 4
Outputs:
- bound_fraction: float32 [64, 32, 128], P('gx', ('gy', 'gz'))
- active_tension: float32 [64, 32, 128], P('gx', ('gy', 'gz'))
Inputs may be any that keep to these rules, and one draw needn't show every extreme that they name: `element_first`: never falling; the cells of each aligned block of 32 cells belong to that block's own 8 elements, each element holding at least one cell. `element_second`: never falling; the cells of each aligned block of 128 cells belong to that block's own 32 elements, each element holding at least one cell. `element_third`: never falling; the cells of each aligned block of 8 cells belong to that block's own 2 elements, each element holding at least one cell.
All inputs are finite; a program needn't handle non-finite values.
Results may differ from a plain program's by a relative error of at most 0.00005.
Values sent between devices are 32-bit elements.
No kernel may reach another device: no remote copies, remote signals or barrier semaphores. Data moves between devices by JAX's collectives and lax.ppermute only.
A program may use at most 64 MiB of HBM per device.

v0:
```python
import jax
import jax.numpy as jnp
from jax import lax
from jax.sharding import PartitionSpec as P

highest = lax.Precision.HIGHEST
step_size = 0.2
bind_rate = 2.0
peak_tension = 2.0
half_square = 0.25


def shifted(x, axis, by):
    length = lax.axis_size(axis)
    pairs = [(i, i + by) for i in range(length) if 0 <= i + by < length]
    return lax.ppermute(x, axis, pairs)


def axis_weights(element, offset, first_node, count, first_cell, cells):
    node_ids = first_node + jnp.arange(count, dtype=jnp.int32)
    inside = element[None, :] == node_ids[:, None]
    following = element[None, :] + 1 == node_ids[:, None]
    raw_weights = jnp.where(inside, 1.0 - offset[None, :], 0.0) + jnp.where(
        following, offset[None, :], 0.0
    )
    scaled = raw_weights / jnp.sum(raw_weights, axis=1, keepdims=True)
    return lax.dynamic_slice_in_dim(scaled, first_cell, cells, 1)


def restrict_block(field, weight_row, weight_depth, weight_col):
    section = jnp.einsum("ai,sizy->sazy", weight_row, field, precision=highest)
    section = jnp.einsum("bz,sazy->saby", weight_depth, section, precision=highest)
    return jnp.einsum("cy,saby->sabc", weight_col, section, precision=highest)


def last_layer(partial_value, dim):
    extent = partial_value.shape[dim]
    return lax.slice_in_dim(partial_value, extent - 1, extent, axis=dim)


def merge_edge(partial_value, incoming, dim):
    extent = partial_value.shape[dim]
    leading = lax.slice_in_dim(partial_value, 0, 1, axis=dim) + incoming
    middle = lax.slice_in_dim(partial_value, 1, extent - 1, axis=dim)
    return lax.concatenate([leading, middle], dim)


def fold_rows(partial_value):
    incoming = shifted(last_layer(partial_value, 2), "gx", 1)
    return merge_edge(partial_value, incoming, 2)


def tension_steps(drivers, troponin, tension, unbind_rate, relax_rate):
    bound = troponin
    active = tension
    for substep in range(drivers.shape[1]):
        calcium_now = drivers[0, substep]
        squared = calcium_now * calcium_now
        binding = squared / (squared + half_square)
        bound = bound + step_size * (bind_rate * binding * (1.0 - bound) - unbind_rate * bound)
        active = active + step_size * relax_rate * (
            peak_tension * drivers[1, substep] * bound - active
        )
    return (bound, active)


def per_device(
    calcium,
    activation,
    element_first,
    offset_first,
    element_second,
    offset_second,
    element_third,
    offset_third,
    troponin,
    tension,
    unbind_rate,
    relax_rate,
):
    sub_count, fine_rows, fine_depth, fine_cols = calcium.shape
    nodes_x, nodes_block, nodes_all_y = troponin.shape
    groups = lax.axis_size("gz")
    row_index = lax.axis_index("gx")
    weight_row = axis_weights(
        element_first,
        offset_first,
        row_index * nodes_x,
        nodes_x + 1,
        row_index * fine_rows,
        fine_rows,
    )
    slab_index = lax.axis_index("gz")
    col_index = lax.axis_index("gy")
    slab_nodes = nodes_block * groups
    nodes_y = nodes_all_y // lax.axis_size("gy")
    weight_depth = axis_weights(
        element_third,
        offset_third,
        slab_index * slab_nodes,
        slab_nodes + 1,
        slab_index * fine_depth,
        fine_depth,
    )
    weight_col = axis_weights(
        element_second,
        offset_second,
        col_index * nodes_y,
        nodes_y + 1,
        col_index * fine_cols,
        fine_cols,
    )
    partial_value = jnp.stack(
        [
            restrict_block(field, weight_row, weight_depth, weight_col)
            for field in (calcium, activation)
        ]
    )
    partial_value = fold_rows(partial_value)
    incoming = shifted(last_layer(partial_value, 3), "gz", 1)
    partial_value = merge_edge(partial_value, incoming, 3)
    incoming = shifted(last_layer(partial_value, 4), "gy", 1)
    partial_value = merge_edge(partial_value, incoming, 4)
    shaped = partial_value.reshape(2, 1, sub_count, nodes_x, groups, nodes_block, nodes_y)
    regrouped = lax.all_to_all(
        lax.all_to_all(shaped, "gz", split_axis=4, concat_axis=1, tiled=True),
        "gy",
        split_axis=1,
        concat_axis=6,
        tiled=True,
    )
    drivers = regrouped.reshape(2, sub_count, nodes_x, nodes_block, nodes_all_y)
    return tension_steps(drivers, troponin, tension, unbind_rate, relax_rate)


def solution(mesh):
    return jax.shard_map(
        per_device,
        mesh=mesh,
        in_specs=(
            P(None, "gx", "gz", "gy"),
            P(None, "gx", "gz", "gy"),
            P(),
            P(),
            P(),
            P(),
            P(),
            P(),
            P("gx", ("gy", "gz"), None),
            P("gx", ("gy", "gz"), None),
            P("gx", ("gy", "gz"), None),
            P("gx", ("gy", "gz"), None),
        ),
        out_specs=(P("gx", ("gy", "gz"), None), P("gx", ("gy", "gz"), None)),
        check_vma=False,
    )
```

profile of v0, /device:TPU:65, one launch (start us, length us, event | category | flops | bytes accessed | tf_op | source)
XLA Modules:
  0.0 76.1 jit_solution(3353908300867582701)
XLA Ops:
  0.6 0.7 broadcast_add_fusion.1
  1.3 0.7 broadcast_subtract_fusion.1
  2.0 0.7 broadcast_add_fusion.2
  2.7 0.7 broadcast_subtract_fusion.2
  3.3 0.7 broadcast_add_fusion
  4.0 0.7 broadcast_subtract_fusion
  4.7 0.9 %fusion.127 = (f32[9]{0:T(128)S(1)}, f32[9,256]{1,0:T(8,128)S(1)}) fusion(f32[256]{0:T(256)} %param.15, s32[256]{0:T(256)S(1)} %broadcast_add_fusion.1, f32[256]{0:T(256)S(1)} %broadcast_subtract_fusion.1, s32[9]{0:T(128)S(1)} %iota_add_fusion.2, s32[256]{0:T(256)} %param.14), kind=kLoop, calls=%fused_computation.170 | loop fusion | flops 13815 | bytes 13384 | tf_op jit(solution)/shard_map/reduce_sum | solution.py:26
  5.6 7.9 %fusion.4 = f32[8,9,32,128]{3,1,2,0:T(8,128)} fusion(f32[8,32,32,128]{3,2,1,0:T(8,128)} %param.12, f32[9,256]{1,0:T(8,128)S(1)} %get-tuple-element.9, s32[]{:T(128)S(6)} %select_n.32, f32[9]{0:T(128)S(1)} %get-tuple-element.8), kind=kOutput, calls=%fused_computation.4 | convolution fusion | flops 113246496 | bytes 5382660 | tf_op jit(solution)/shard_map/ai,sizy->sazy/dot_general | solution.py:31
  13.5 4.4 %fusion.7 = f32[8,9,32,128]{3,1,2,0:T(8,128)S(1)} fusion(f32[8,32,32,128]{3,2,1,0:T(8,128)S(1)} %copy-done, f32[9,256]{1,0:T(8,128)S(1)} %get-tuple-element.9, s32[]{:T(128)S(6)} %select_n.32, f32[9]{0:T(128)S(1)} %get-tuple-element.8), kind=kOutput, calls=%fused_computation.5 | convolution fusion | flops 113246496 | bytes 5382660 | tf_op jit(solution)/shard_map/ai,sizy->sazy/dot_general | solution.py:31
  18.2 2.6 %convolution_bitcast_fusion.3 = f32[8,9,9,128]{3,2,1,0:T(8,128)S(1)} fusion(f32[8,9,32,128]{3,1,2,0:T(8,128)} %fusion.4, f32[9,128]{1,0:T(8,128)S(1)} %get-tuple-element.11, s32[]{:T(128)S(6)} %select_n.35, f32[9]{0:T(128)S(1)} %get-tuple-element.10), kind=kOutput, calls=%fused_computation.9 | convolution fusion | flops 31850784 | bytes 1516072 | tf_op jit(solution)/shard_map/bz,sazy->saby/dot_general | solution.py:32
  20.8 1.1 %convolution_bitcast_fusion.1 = f32[8,9,9,128]{3,2,1,0:T(8,128)S(1)} fusion(f32[8,9,32,128]{3,1,2,0:T(8,128)S(1)} %fusion.7, f32[9,128]{1,0:T(8,128)S(1)} %get-tuple-element.11, s32[]{:T(128)S(6)} %select_n.35, f32[9]{0:T(128)S(1)} %get-tuple-element.10), kind=kOutput, calls=%fused_computation.7 | convolution fusion | flops 31850784 | bytes 1516072 | tf_op jit(solution)/shard_map/bz,sazy->saby/dot_general | solution.py:32
  22.1 0.9 %convolution_bitcast_fusion.2 = f32[1,8,9,9,33]{4,3,2,1,0:T(8,128)S(1)} fusion(f32[8,9,9,128]{3,2,1,0:T(8,128)S(1)} %convolution_bitcast_fusion.3, f32[33,512]{1,0:T(8,128)S(1)} %get-tuple-element.7, s32[]{:T(128)S(6)} %select_n.38, f32[33]{0:T(128)S(1)} %get-tuple-element.6), kind=kOutput, calls=%fused_computation.8 | convolution fusion | flops 32850048 | bytes 696356 | tf_op jit(solution)/shard_map/cy,saby->sabc/dot_general | solution.py:33
  22.9 0.7 convolution_bitcast_fusion
  23.7 3.1 %collective-permute-start = (f32[2,8,1,9,33]{4,3,2,1,0:T(8,128)S(1)}, f32[2,8,1,9,33]{4,3,2,1,0:T(8,128)S(1)}, u32[]{:S(2)}, u32[]{:S(2)}) collective-permute-start(f32[2,8,1,9,33]{4,3,2,1,0:T(8,128)S(1)} %pad_maximum_fusion), channel_id=1, source_target_pairs={{0,16},{16,32},{32,48},{48,64},{64,80},{80,96},{96,112},{1,17},{17... | collective-permute-start | bytes 57032 | tf_op jit(solution)/shard_map/ppermute | solution.py:16
  26.8 6.8 %collective-permute-done = f32[2,8,1,9,33]{4,3,2,1,0:T(8,128)S(1)} collective-permute-done((f32[2,8,1,9,33]{4,3,2,1,0:T(8,128)S(1)}, f32[2,8,1,9,33]{4,3,2,1,0:T(8,128)S(1)}, u32[]{:S(2)}, u32[]{:S(2)}) %collective-permute-start) | collective-permute-done | bytes 19040 | tf_op jit(solution)/shard_map/ppermute | solution.py:16
  33.7 3.2 %collective-permute-start.1 = (f32[2,8,8,1,33]{4,3,2,1,0:T(1,128)S(1)}, f32[2,8,8,1,33]{4,3,2,1,0:T(1,128)S(1)}, u32[]{:S(2)}, u32[]{:S(2)}) collective-permute-start(f32[2,8,8,1,33]{4,3,2,1,0:T(1,128)S(1)} %slice.101), channel_id=1, source_target_pairs={{0,1},{1,2},{2,3},{4,5},{5,6},{6,7},{8,9},{9,10},{10,11},{12,13},{... | collective-permute-start | bytes 50696 | tf_op jit(solution)/shard_map/ppermute | solution.py:16
  37.0 1.3 %collective-permute-done.1 = f32[2,8,8,1,33]{4,3,2,1,0:T(1,128)S(1)} collective-permute-done((f32[2,8,8,1,33]{4,3,2,1,0:T(1,128)S(1)}, f32[2,8,8,1,33]{4,3,2,1,0:T(1,128)S(1)}, u32[]{:S(2)}, u32[]{:S(2)}) %collective-permute-start.1) | collective-permute-done | bytes 16928 | tf_op jit(solution)/shard_map/ppermute | solution.py:16
  38.7 5.5 %collective-permute-start.2 = (f32[2,8,8,8,1]{4,3,2,1,0:T(8,128)S(1)}, f32[2,8,8,8,1]{4,3,2,1,0:T(8,128)S(1)}, u32[]{:S(2)}, u32[]{:S(2)}) collective-permute-start(f32[2,8,8,8,1]{4,3,2,1,0:T(8,128)S(1)} %fusion.13), channel_id=1, source_target_pairs={{0,4},{4,8},{8,12},{1,5},{5,9},{9,13},{2,6},{6,10},{10,14},{3,7},{... | collective-permute-start | bytes 12296 | tf_op jit(solution)/shard_map/ppermute | solution.py:16
  44.2 6.1 %collective-permute-done.2 = f32[2,8,8,8,1]{4,3,2,1,0:T(8,128)S(1)} collective-permute-done((f32[2,8,8,8,1]{4,3,2,1,0:T(8,128)S(1)}, f32[2,8,8,8,1]{4,3,2,1,0:T(8,128)S(1)}, u32[]{:S(2)}, u32[]{:S(2)}) %collective-permute-start.2) | collective-permute-done | bytes 4128 | tf_op jit(solution)/shard_map/ppermute | solution.py:16
  51.4 9.6 %all_to_all.33 = f32[4,1,8192]{2,1,0:T(1,128)S(1)} all-to-all(f32[4,1,8192]{2,1,0:T(1,128)S(1)} %reshape.73), channel_id=1, replica_groups=mesh['gx'=8,'gy'=4,'gz'=4] {'gz'}, dimensions={0} | all-to-all | bytes 262144 | tf_op jit(solution)/shard_map/all_to_all | solution.py:126
  61.5 1.0 %reduce = f32[4,8192]{1,0:T(4,128)S(1)} reduce(f32[4,1,8192]{2,1,0:T(1,128)S(1)} %all_to_all.33, f32[]{:T(128)} %broadcast.223), dimensions={1}, to_apply=%all_to_all.24.reduce_sub_computation | reduce | bytes 262148 | tf_op jit(solution)/shard_map/all_to_all | solution.py:126
  63.6 9.1 %all_to_all.34 = f32[4,1,8192]{2,1,0:T(1,128)S(1)} all-to-all(f32[4,1,8192]{2,1,0:T(1,128)S(1)} %reshape.75), channel_id=1, replica_groups=mesh['gx'=8,'gy'=4,'gz'=4] {'gy'}, dimensions={0} | all-to-all | bytes 262144 | tf_op jit(solution)/shard_map/all_to_all | solution.py:125
  72.7 1.0 %reduce.1 = f32[4,8192]{1,0:T(4,128)S(1)} reduce(f32[4,1,8192]{2,1,0:T(1,128)S(1)} %all_to_all.34, f32[]{:T(128)} %broadcast.223), dimensions={1}, to_apply=%all_to_all.28.reduce_sub_computation | reduce | bytes 262148 | tf_op jit(solution)/shard_map/all_to_all | solution.py:125
  74.9 0.6 copy.38
  (44 shorter events, 5.5 us)
Async XLA Ops:
  5.6 7.9 %copy-start = (f32[8,32,32,128]{3,2,1,0:T(8,128)S(1)}, f32[8,32,32,128]{3,2,1,0:T(8,128)}, u32[]{:S(2)}) copy-start(f32[8,32,32,128]{3,2,1,0:T(8,128)} %param.13) | copy-start | bytes 12582916
  13.5 4.4 %copy-start.7 = (f32[128]{0:T(128)S(1)}, f32[128]{0:T(128)}, u32[]{:S(2)}) copy-start(f32[128]{0:T(128)} %param.19) | copy-start | bytes 1540
  13.5 4.4 %copy-start.8 = (s32[128]{0:T(128)S(1)}, s32[128]{0:T(128)}, u32[]{:S(2)}) copy-start(s32[128]{0:T(128)} %param.18) | copy-start | bytes 1540
  17.9 3.9 %copy-start.5 = (f32[512]{0:T(512)S(1)}, f32[512]{0:T(512)}, u32[]{:S(2)}) copy-start(f32[512]{0:T(512)} %param.17) | copy-start | bytes 6148
  17.9 3.9 %copy-start.6 = (s32[512]{0:T(512)S(1)}, s32[512]{0:T(512)}, u32[]{:S(2)}) copy-start(s32[512]{0:T(512)} %param.16) | copy-start | bytes 6148
  23.7 9.9 %collective-permute-start = (f32[2,8,1,9,33]{4,3,2,1,0:T(8,128)S(1)}, f32[2,8,1,9,33]{4,3,2,1,0:T(8,128)S(1)}, u32[]{:S(2)}, u32[]{:S(2)}) collective-permute-start(f32[2,8,1,9,33]{4,3,2,1,0:T(8,128)S(1)} %pad_maximum_fusion), channel_id=1, source_target_pairs={{0,16},{16,32},{32,48},{48,64},{64,80},{80,96},{96,112},{1,17},{17... | collective-permute-start | bytes 57032 | tf_op jit(solution)/shard_map/ppermute | solution.py:16
  33.7 4.5 %collective-permute-start.1 = (f32[2,8,8,1,33]{4,3,2,1,0:T(1,128)S(1)}, f32[2,8,8,1,33]{4,3,2,1,0:T(1,128)S(1)}, u32[]{:S(2)}, u32[]{:S(2)}) collective-permute-start(f32[2,8,8,1,33]{4,3,2,1,0:T(1,128)S(1)} %slice.101), channel_id=1, source_target_pairs={{0,1},{1,2},{2,3},{4,5},{5,6},{6,7},{8,9},{9,10},{10,11},{12,13},{... | collective-permute-start | bytes 50696 | tf_op jit(solution)/shard_map/ppermute | solution.py:16
  38.7 11.6 %collective-permute-start.2 = (f32[2,8,8,8,1]{4,3,2,1,0:T(8,128)S(1)}, f32[2,8,8,8,1]{4,3,2,1,0:T(8,128)S(1)}, u32[]{:S(2)}, u32[]{:S(2)}) collective-permute-start(f32[2,8,8,8,1]{4,3,2,1,0:T(8,128)S(1)} %fusion.13), channel_id=1, source_target_pairs={{0,4},{4,8},{8,12},{1,5},{5,9},{9,13},{2,6},{6,10},{10,14},{3,7},{... | collective-permute-start | bytes 12296 | tf_op jit(solution)/shard_map/ppermute | solution.py:16
  63.6 11.2 %copy-start.1 = (f32[8,2,128]{2,1,0:T(2,128)S(1)}, f32[8,2,128]{2,1,0:T(2,128)}, u32[]{:S(2)}) copy-start(f32[8,2,128]{2,1,0:T(2,128)} %param.21) | copy-start | bytes 24580
  63.6 11.2 %copy-start.2 = (f32[8,2,128]{2,1,0:T(2,128)S(1)}, f32[8,2,128]{2,1,0:T(2,128)}, u32[]{:S(2)}) copy-start(f32[8,2,128]{2,1,0:T(2,128)} %param.23) | copy-start | bytes 24580
  63.6 11.2 %copy-start.3 = (f32[8,2,128]{2,1,0:T(2,128)S(1)}, f32[8,2,128]{2,1,0:T(2,128)}, u32[]{:S(2)}) copy-start(f32[8,2,128]{2,1,0:T(2,128)} %param.22) | copy-start | bytes 24580
  63.6 11.2 %copy-start.4 = (f32[8,2,128]{2,1,0:T(2,128)S(1)}, f32[8,2,128]{2,1,0:T(2,128)}, u32[]{:S(2)}) copy-start(f32[8,2,128]{2,1,0:T(2,128)} %param.20) | copy-start | bytes 24580
where the time goes:
time: 76.9 us; the launch traced here: 76.1 us
  blocking collectives  18.7 us (24%)
  matrix products  17.6 us (23%)
  waiting for transfers between devices  14.1 us (18%)
  starting transfers between devices  11.8 us (15%)
  other arithmetic  8.23 us (11%)
  local copies, waits for them, and re-layouts  4.72 us (6%)
  between operations  0.96 us (1%)
    ppermute x3, waiting for transfers between devices, shifted(): return lax.ppermute(x, axis, pairs)  14.1 us
    dot_general x2, matrix products, restrict_block(): section = jnp.einsum('ai,sizy->sazy', weight_row, field, precision=highest)  12.3 us
    ppermute x3, starting transfers between devices, shifted(): return lax.ppermute(x, axis, pairs)  11.8 us
    all_to_all x1, blocking collectives, per_device(): lax.all_to_all(shaped, 'gz', split_axis=4, concat_axis=1, tiled=True)  9.6 us
    all_to_all x1, blocking collectives, per_device(): lax.all_to_all(lax.all_to_all(shaped, 'gz', split_axis=4, concat_axis=1,...  9.07 us
    dot_general x2, matrix products, restrict_block(): jnp.einsum('bz,sazy->saby', weight_depth, section, precision=highest)  3.69 us
    unnamed x25, local copies, waits for them, and re-layouts  3.29 us
    add x3, other arithmetic, axis_weights(): following = element[None, :] + 1 == node_ids[:, None]  2.02 us
  transfers between devices with their start and end apart: 3, of which 3 were waited for; matrix products, arithmetic and copies ran while one was open for 0% of the time, Pallas kernels for 0%

commit v1 on v0

v1 whole, which is shorter than its diff:
```python
import jax
import jax.numpy as jnp
from jax import lax
from jax.experimental import pallas as pl
from jax.experimental.pallas import tpu as pltpu
from jax.sharding import PartitionSpec as P

step_size = 0.2
bind_rate = 2.0
peak_tension = 2.0
half_square = 0.25

f32 = jnp.float32
bf16 = jnp.bfloat16
LANES = 128
SUBS = 8
NODES = 8
COLS = 32
ROWS = 88
BLOCK = 104
PIECE = 72


def hat(element, offset, first_node, rows):
    cells = element.shape[0]
    element = element.reshape(1, cells)
    offset = offset.reshape(1, cells)
    node = first_node + lax.broadcasted_iota(jnp.int32, (rows, cells), 0)
    raw = jnp.where(element == node, 1.0 - offset, 0.0) + jnp.where(
        element + 1 == node, offset, 0.0
    )
    return raw / jnp.sum(raw, axis=1, keepdims=True)


def halves(value):
    high = value.astype(bf16).astype(f32)
    return high, value - high


def lane_ids(rows):
    return lax.broadcasted_iota(jnp.int32, (rows, LANES), 1)


def pick_lanes(values, index):
    return jnp.take_along_axis(values, index, axis=1, mode="promise_in_bounds")


def restrict_kernel(
    calcium,
    activation,
    element_first,
    offset_first,
    element_second,
    offset_second,
    element_third,
    offset_third,
    blocks,
    edge,
    pair_weight,
    col_high,
    col_low,
    partials,
    packed,
):
    step = pl.program_id(0)
    gx, gy, gz = lax.axis_index("gx"), lax.axis_index("gy"), lax.axis_index("gz")

    @pl.when(step == 0)
    def _():
        first = hat(element_first[...], offset_first[...], gx * NODES, 16)
        own = jnp.where(gx >= 4, first[:, LANES:], first[:, :LANES])
        third = hat(element_third[...], offset_third[...], gz * NODES, 16)
        lane = lane_ids(16)
        depth = pick_lanes(third, gz * 32 + lane % 32)
        for tile in range(8):
            row = pick_lanes(own, lax.rem(gx, 4) * 32 + 4 * tile + lane // 32)
            parts = [depth[b : b + 1] * row[:NODES] for b in range(NODES + 1)]
            parts.append(row[NODES : NODES + 1] * depth[:NODES])
            corner = row[NODES : NODES + 1] * depth[NODES : NODES + 1]
            top = lax.broadcasted_iota(jnp.int32, (8, LANES), 0) == 0
            parts.append(jnp.where(top, corner, 0.0))
            both = jnp.concatenate(halves(jnp.concatenate(parts, 0)), 0)
            pair_weight[:, tile * LANES : (tile + 1) * LANES] = both.astype(bf16)

    @pl.when(step == 2)
    def _():
        second = hat(element_second[...], offset_second[...], gy * COLS, 40)
        own = second[:, :LANES]
        for chunk in range(1, 4):
            piece = second[:, chunk * LANES : (chunk + 1) * LANES]
            own = jnp.where(gy == chunk, piece, own)
        full = jnp.concatenate([own, jnp.zeros((LANES - 40, LANES), f32)], 0)
        turned = full.T
        lane = lane_ids(LANES)
        for group in range(4):
            start = group * COLS
            main = turned if start == 0 else pltpu.roll(turned, start, 1)
            main = jnp.where(lane // COLS == group, main, 0.0)
            shift = (start - COLS) % LANES
            extra = turned if shift == 0 else pltpu.roll(turned, shift, 1)
            extra = jnp.where(lane == start, extra, 0.0)
            high, low = halves(jnp.concatenate([main, extra], 1))
            rows = slice(group * LANES, (group + 1) * LANES)
            col_high[rows] = high.astype(bf16)
            col_low[rows] = low.astype(bf16)

    cells = 32 * 32
    field = jnp.concatenate(
        [calcium[0].reshape(cells, LANES), activation[0].reshape(cells, LANES)], 1
    )
    high, low = halves(field)
    upper = jnp.dot(pair_weight[...], high.astype(bf16), preferred_element_type=f32)
    lower = jnp.dot(pair_weight[:96], low.astype(bf16), preferred_element_type=f32)
    section = upper[:ROWS] + upper[ROWS:] + lower[:ROWS]
    group = lax.rem(step, 4)
    partials[group, :ROWS] = section[:, :LANES]
    partials[group, ROWS:] = section[:, LANES:]

    def columns():
        whole = jnp.concatenate([partials[g] for g in range(4)], 1)
        high, low = halves(whole)
        high, low = high.astype(bf16), low.astype(bf16)
        return (
            jnp.dot(high, col_high[...], preferred_element_type=f32)
            + jnp.dot(low, col_high[...], preferred_element_type=f32)
            + jnp.dot(high, col_low[...], preferred_element_type=f32)
        )

    @pl.when(step == 3)
    def _():
        packed[...] = columns()

    @pl.when(step == SUBS - 1)
    def _():
        first, last = packed[...], columns()
        quads = [first[:ROWS], last[:ROWS], first[ROWS:], last[ROWS:]]
        main = [q[:, :LANES] for q in quads]
        extra = quads[0][:, LANES:]
        for j in range(1, 4):
            extra = extra + pltpu.roll(quads[j][:, LANES:], j, 1)
        for k in range(4):
            tail = None
            for p, plane in enumerate((2 * k, 2 * k + 1, NODES)):
                rows = slice(plane * 8, plane * 8 + 8)
                for j in range(4):
                    start = j * 24 + p * 8
                    blocks[k, start : start + 8] = main[j][rows]
                piece = extra[rows]
                piece = piece if p == 0 else pltpu.roll(piece, 4 * p, 1)
                tail = piece if tail is None else tail + piece
            blocks[k, 96:104] = tail
        for j in range(4):
            edge[j * 8 : j * 8 + 8] = main[j][72:80]
        corners = [m[80:81] for m in main] + [extra[80:81]]
        edge[32:40] = jnp.concatenate(corners + [jnp.zeros((3, LANES), f32)], 0)
        edge[40:48] = extra[72:80]


def route_kernel(blocks, incoming, *outs):
    gz = lax.axis_index("gz")
    top = lax.broadcasted_iota(jnp.int32, (8, LANES), 0) == 0
    for k in range(4):
        which = lax.rem(gz + k, 4)
        out = outs[k]
        tail = None
        for p in range(3):
            for j in range(4):
                start = j * 24 + p * 8
                if p < 2:
                    row = incoming[pl.ds(j * 8 + 2 * which + p, 1), :]
                else:
                    row = incoming[32 + j : 33 + j, :]
                out[start : start + 8] = blocks[which, start : start + 8] + jnp.where(
                    top, row, 0.0
                )
            if p < 2:
                row = incoming[pl.ds(40 + 2 * which + p, 1), :]
            else:
                row = incoming[36:37, :]
            row = jnp.where(top, row, 0.0)
            row = row if p == 0 else pltpu.roll(row, 4 * p, 1)
            tail = row if tail is None else tail + row
        out[96:104] = blocks[which, 96:104] + tail


def combine_kernel(own, one, two, three, *rest):
    outs, slabs = rest[:4], rest[4]
    gy, gz = lax.axis_index("gy"), lax.axis_index("gz")
    for k, message in enumerate((own, one, two, three)):
        slabs[lax.rem(gz + 4 - k, 4)] = message[...]
    lane = lane_ids(8)
    for k in range(4):
        slab = lax.rem(gy + k, 4)
        before = lax.rem(slab + 3, 4)
        joins = jnp.logical_and(gz == 0, slab > 0)
        out = outs[k]
        for j in range(4):
            start = j * 24
            plane = slabs[before, start + 16 : start + 24]
            out[j * 16 : j * 16 + 8] = slabs[slab, start : start + 8] + jnp.where(
                joins, plane, 0.0
            )
            out[j * 16 + 8 : j * 16 + 16] = slabs[slab, start + 8 : start + 16]
        tail = pltpu.roll(slabs[before, 96:104], LANES - 8, 1)
        tail = jnp.where(jnp.logical_and(joins, lane % COLS < 4), tail, 0.0)
        out[64:72] = slabs[slab, 96:104] + tail


def tension_kernel(
    own, one, two, three, troponin, tension, unbind, relax, bound_out, active_out, chunks
):
    gy = lax.axis_index("gy")
    for k, message in enumerate((own, one, two, three)):
        chunks[lax.rem(gy + 4 - k, 4)] = message[...]
    lane = lane_ids(8)
    pieces = [chunks[c] for c in range(4)]

    def turn(value, shift):
        shift = shift % LANES
        return value if shift == 0 else pltpu.roll(value, shift, 1)

    def drive(f, substep, plane):
        half, group = divmod(substep, 4)
        j = 2 * f + half
        start = j * 16 + plane * 8
        total = None
        for c in range(4):
            part = turn(pieces[c][start : start + 8], COLS * (c - group))
            total = part if total is None else jnp.where(lane // COLS == c, part, total)
        for c in range(3):
            shift = COLS * (c + 1) - (COLS * group + 4 * plane + j)
            part = turn(pieces[c][64:72], shift)
            total = total + jnp.where(lane == COLS * (c + 1), part, 0.0)
        return total

    for plane in range(2):
        bound = troponin[:, plane, :]
        active = tension[:, plane, :]
        unbinding = unbind[:, plane, :]
        relaxing = step_size * relax[:, plane, :]
        for substep in range(SUBS):
            calcium_now = drive(0, substep, plane)
            squared = calcium_now * calcium_now
            binding = squared / (squared + half_square)
            bound = bound + step_size * (
                bind_rate * binding * (1.0 - bound) - unbinding * bound
            )
            active = active + relaxing * (
                peak_tension * drive(1, substep, plane) * bound - active
            )
        bound_out[:, plane, :] = bound
        active_out[:, plane, :] = active


def exchange(messages, axis):
    received = [messages[0]]
    for k in range(1, 4):
        pairs = [(i, (i + k) % 4) for i in range(4)]
        received.append(lax.ppermute(messages[k], axis, pairs))
    return received


def per_device(
    calcium,
    activation,
    element_first,
    offset_first,
    element_second,
    offset_second,
    element_third,
    offset_third,
    troponin,
    tension,
    unbind_rate,
    relax_rate,
):
    field_spec = pl.BlockSpec((1, 32, 32, LANES), lambda s: (s, 0, 0, 0))
    line = lambda n: pl.BlockSpec((n,), lambda s: (0,))
    blocks, edge = pl.pallas_call(
        restrict_kernel,
        grid=(SUBS,),
        in_specs=[
            field_spec,
            field_spec,
            line(256),
            line(256),
            line(512),
            line(512),
            line(128),
            line(128),
        ],
        out_specs=[
            pl.BlockSpec((4, BLOCK, LANES), lambda s: (0, 0, 0)),
            pl.BlockSpec((48, LANES), lambda s: (0, 0)),
        ],
        out_shape=[
            jax.ShapeDtypeStruct((4, BLOCK, LANES), f32),
            jax.ShapeDtypeStruct((48, LANES), f32),
        ],
        scratch_shapes=[
            pltpu.VMEM((2 * ROWS, 1024), bf16),
            pltpu.VMEM((512, 256), bf16),
            pltpu.VMEM((512, 256), bf16),
            pltpu.VMEM((4, 2 * ROWS, LANES), f32),
            pltpu.VMEM((2 * ROWS, 256), f32),
        ],
        compiler_params=pltpu.CompilerParams(dimension_semantics=("arbitrary",)),
        name="restrict",
    )(
        calcium,
        activation,
        element_first,
        offset_first,
        element_second,
        offset_second,
        element_third,
        offset_third,
    )
    incoming = lax.ppermute(edge, "gx", [(i, i + 1) for i in range(7)])
    message = jax.ShapeDtypeStruct((BLOCK, LANES), f32)
    messages = pl.pallas_call(route_kernel, out_shape=[message] * 4, name="route")(
        blocks, incoming
    )
    messages = exchange(messages, "gz")
    piece = jax.ShapeDtypeStruct((PIECE, LANES), f32)
    pieces = pl.pallas_call(
        combine_kernel,
        out_shape=[piece] * 4,
        scratch_shapes=[pltpu.VMEM((4, BLOCK, LANES), f32)],
        name="combine",
    )(*messages)
    pieces = exchange(pieces, "gy")
    result = jax.ShapeDtypeStruct(troponin.shape, f32)
    return pl.pallas_call(
        tension_kernel,
        out_shape=[result, result],
        scratch_shapes=[pltpu.VMEM((4, PIECE, LANES), f32)],
        name="tension",
    )(*pieces, troponin, tension, unbind_rate, relax_rate)


def solution(mesh):
    node_spec = P("gx", ("gy", "gz"), None)
    return jax.shard_map(
        per_device,
        mesh=mesh,
        in_specs=(P(None, "gx", "gz", "gy"),) * 2 + (P(),) * 6 + (node_spec,) * 4,
        out_specs=(node_spec, node_spec),
        check_vma=False,
    )
```

time: 76.9 us -> 40.8 us (0.53)
  blocking collectives: 18.7 us -> 0 us
  matrix products: 17.6 us -> 0 us
  Pallas kernels: 0 us -> 13.9 us
  other arithmetic: 8.23 us -> 0 us
  waiting for transfers between devices: 14.1 us -> 10.8 us
  local copies, waits for them, and re-layouts: 4.72 us -> 1.83 us
  starting transfers between devices: 11.8 us -> 13.2 us
    all_to_all x2 -> x0, blocking collectives: 18.7 us -> none  [the longest x1 9.6 us: per_device(): lax.all_to_all(shaped, 'gz', split_axis=4, concat_axis=1, tiled=True)]
    dot_general x6 -> x0, matrix products: 17.6 us -> none  [the longest x2 12.3 us: restrict_block(): section = jnp.einsum('ai,sizy->sazy', weight_row, field, precision=highest)]
    pallas_call x0 -> x4, Pallas kernels: none -> 13.9 us  [the longest x1 8.85 us: per_device(): pl.pallas_call(restrict_kernel, grid=(SUBS,), in_specs=[field_spec, field...]
    ppermute x3 -> x7, waiting for transfers between devices: 14.1 us -> 10.8 us  [the longest x6 5.49 us: exchange(): received.append(lax.ppermute(messages[k], axis, pairs))]
    add x10 -> x0, other arithmetic: 2.33 us -> none  [the longest x3 2.02 us: axis_weights(): following = element[None, :] + 1 == node_ids[:, None]]
    sub x3 -> x0, other arithmetic: 2.02 us -> none  [axis_weights(): 1.0 - offset[None, :]]
    all_to_all x2 -> x0, other arithmetic: 1.96 us -> none  [the longest x1 0.98 us: per_device(): lax.all_to_all(lax.all_to_all(shaped, 'gz', split_axis=4, concat_axis=1,...]
    unnamed x25 -> x14, local copies, waits for them, and re-layouts: 3.29 us -> 1.83 us
  transfers between devices with their start and end apart: 3 -> 7, of which waited for: 3 -> 6; matrix products, arithmetic and copies ran while one was open for 0% -> 0% of each run, Pallas kernels for 0% -> 0%
where the time goes in v1:
time: 40.8 us; the launch traced here: 40.4 us
  Pallas kernels  13.9 us (34%)
  starting transfers between devices  13.2 us (32%)
  waiting for transfers between devices  10.8 us (26%)
  local copies, waits for them, and re-layouts  1.83 us (4%)
  between operations  0.66 us (2%)
    ppermute x6, starting transfers between devices, exchange(): received.append(lax.ppermute(messages[k], axis, pairs))  10.1 us
    pallas_call x1, Pallas kernels, per_device(): pl.pallas_call(restrict_kernel, grid=(SUBS,), in_specs=[field_spec, field...  8.85 us
    ppermute x6, waiting for transfers between devices, exchange(): received.append(lax.ppermute(messages[k], axis, pairs))  5.49 us
    ppermute x1, waiting for transfers between devices, per_device(): incoming = lax.ppermute(edge, 'gx', [(i, i + 1) for i in range(7)])  5.28 us
    ppermute x1, starting transfers between devices, per_device(): incoming = lax.ppermute(edge, 'gx', [(i, i + 1) for i in range(7)])  3.09 us
    unnamed x14, local copies, waits for them, and re-layouts  1.83 us
    pallas_call x1, Pallas kernels, per_device(): pl.pallas_call(tension_kernel, out_shape=[result, result], scratch_shapes...  1.74 us
    pallas_call x1, Pallas kernels, per_device(): pl.pallas_call(route_kernel, out_shape=[message] * 4, name='route')  1.69 us
  transfers between devices with their start and end apart: 7, of which 6 were waited for; matrix products, arithmetic and copies ran while one was open for 0% of the time, Pallas kernels for 0%

profile of v1, /device:TPU:65, one launch (start us, length us, event | category | flops | bytes accessed | tf_op | source)
XLA Modules:
  0.0 40.4 jit_solution(17768288948103246955)
XLA Ops:
  0.6 8.9 %restrict.1 = (f32[4,104,128]{2,1,0:T(8,128)}, f32[48,128]{1,0:T(8,128)}) custom-call(f32[8,32,32,128]{3,2,1,0:T(8,128)} %calcium.1, f32[8,32,32,128]{3,2,1,0:T(8,128)} %activation.1, s32[256]{0:T(256)} %element_first.1, f32[256]{0:T(256)} %offset_first.1, s32[512]{0:T(512)} %element_second.1, f32[512]{0:T(512)} %offset_second.1, s32[128]{0:T(128)} %element_third.1, ...), custom_call_target="tpu_custom_call" | custom-call | tf_op jit(solution)/shard_map/restrict/pallas_call | solution.py:279
  9.5 3.1 %collective-permute-start = (f32[48,128]{1,0:T(8,128)}, f32[48,128]{1,0:T(8,128)S(1)}, u32[]{:S(2)}, u32[]{:S(2)}) collective-permute-start(f32[48,128]{1,0:T(8,128)} %get-tuple-element.13), channel_id=1, source_target_pairs={{0,16},{16,32},{32,48},{48,64},{64,80},{80,96},{96,112},{1,17},{17... | collective-permute-start | bytes 73736 | tf_op jit(solution)/shard_map/ppermute | solution.py:319
  12.6 5.3 %collective-permute-done.incoming = f32[48,128]{1,0:T(8,128)S(1)} collective-permute-done((f32[48,128]{1,0:T(8,128)}, f32[48,128]{1,0:T(8,128)S(1)}, u32[]{:S(2)}, u32[]{:S(2)}) %collective-permute-start) | collective-permute-done | bytes 24608 | tf_op jit(solution)/shard_map/ppermute | solution.py:319
  17.9 0.6 %copy-done.6 = f32[48,128]{1,0:T(8,128)} copy-done((f32[48,128]{1,0:T(8,128)}, f32[48,128]{1,0:T(8,128)S(1)}, u32[]{:S(2)}) %copy-start.6) | copy-done | bytes 24600
  18.5 1.7 %route.1 = (f32[104,128]{1,0:T(8,128)}, f32[104,128]{1,0:T(8,128)}, f32[104,128]{1,0:T(8,128)}, f32[104,128]{1,0:T(8,128)}) custom-call(f32[4,104,128]{2,1,0:T(8,128)} %get-tuple-element.12.blocks, f32[48,128]{1,0:T(8,128)} %copy-done.6), custom_call_target="tpu_custom_call" | custom-call | tf_op jit(solution)/shard_map/route/pallas_call | solution.py:321
  20.2 1.3 %collective-permute-start.1 = (f32[104,128]{1,0:T(8,128)}, f32[104,128]{1,0:T(8,128)S(1)}, u32[]{:S(2)}, u32[]{:S(2)}) collective-permute-start(f32[104,128]{1,0:T(8,128)} %get-tuple-element.15), channel_id=1, source_target_pairs={{0,1},{1,2},{2,3},{3,0},{4,5},{5,6},{6,7},{7,4},{8,9},{9,10},{10,1... | collective-permute-start | bytes 159752 | tf_op jit(solution)/shard_map/ppermute | solution.py:259
  21.5 2.6 %collective-permute-start.2 = (f32[104,128]{1,0:T(8,128)}, f32[104,128]{1,0:T(8,128)S(1)}, u32[]{:S(2)}, u32[]{:S(2)}) collective-permute-start(f32[104,128]{1,0:T(8,128)} %get-tuple-element.16), channel_id=1, source_target_pairs={{0,2},{1,3},{2,0},{3,1},{4,6},{5,7},{6,4},{7,5},{8,10},{9,11},{10,... | collective-permute-start | bytes 159752 | tf_op jit(solution)/shard_map/ppermute | solution.py:259
  24.1 1.1 %collective-permute-start.3 = (f32[104,128]{1,0:T(8,128)}, f32[104,128]{1,0:T(8,128)S(1)}, u32[]{:S(2)}, u32[]{:S(2)}) collective-permute-start(f32[104,128]{1,0:T(8,128)} %get-tuple-element.17), channel_id=1, source_target_pairs={{0,3},{1,0},{2,1},{3,2},{4,7},{5,4},{6,5},{7,6},{8,11},{9,8},{10,9... | collective-permute-start | bytes 159752 | tf_op jit(solution)/shard_map/ppermute | solution.py:259
  25.1 0.0 collective-permute-done.1.one
  25.1 1.2 %collective-permute-done.2.two = f32[104,128]{1,0:T(8,128)S(1)} collective-permute-done((f32[104,128]{1,0:T(8,128)}, f32[104,128]{1,0:T(8,128)S(1)}, u32[]{:S(2)}, u32[]{:S(2)}) %collective-permute-start.2) | collective-permute-done | bytes 53280 | tf_op jit(solution)/shard_map/ppermute | solution.py:259
  26.4 1.0 %collective-permute-done.3.three = f32[104,128]{1,0:T(8,128)S(1)} collective-permute-done((f32[104,128]{1,0:T(8,128)}, f32[104,128]{1,0:T(8,128)S(1)}, u32[]{:S(2)}, u32[]{:S(2)}) %collective-permute-start.3) | collective-permute-done | bytes 53280 | tf_op jit(solution)/shard_map/ppermute | solution.py:259
  27.4 0.0 copy-done
  27.4 0.0 copy-done.1
  27.4 0.6 %copy-done.2 = f32[104,128]{1,0:T(8,128)} copy-done((f32[104,128]{1,0:T(8,128)}, f32[104,128]{1,0:T(8,128)S(1)}, u32[]{:S(2)}) %copy-start.2) | copy-done | bytes 53272
  28.0 1.6 %combine.1 = (f32[72,128]{1,0:T(8,128)}, f32[72,128]{1,0:T(8,128)}, f32[72,128]{1,0:T(8,128)}, f32[72,128]{1,0:T(8,128)}) custom-call(f32[104,128]{1,0:T(8,128)} %get-tuple-element.14.own, f32[104,128]{1,0:T(8,128)} %copy-done, f32[104,128]{1,0:T(8,128)} %copy-done.1, f32[104,128]{1,0:T(8,128)} %copy-done.2), custom_call_target="tpu_custom_call" | custom-call | tf_op jit(solution)/shard_map/combine/pallas_call | solution.py:326
  29.7 4.6 %collective-permute-start.4 = (f32[72,128]{1,0:T(8,128)}, f32[72,128]{1,0:T(8,128)S(1)}, u32[]{:S(2)}, u32[]{:S(2)}) collective-permute-start(f32[72,128]{1,0:T(8,128)} %get-tuple-element.19), channel_id=1, source_target_pairs={{0,4},{4,8},{8,12},{12,0},{1,5},{5,9},{9,13},{13,1},{2,6},{6,10},{... | collective-permute-start | bytes 110600 | tf_op jit(solution)/shard_map/ppermute | solution.py:259
  34.3 0.1 collective-permute-start.5
  34.4 0.3 collective-permute-start.6
  34.8 0.9 %collective-permute-done.4.one = f32[72,128]{1,0:T(8,128)S(1)} collective-permute-done((f32[72,128]{1,0:T(8,128)}, f32[72,128]{1,0:T(8,128)S(1)}, u32[]{:S(2)}, u32[]{:S(2)}) %collective-permute-start.4) | collective-permute-done | bytes 36896 | tf_op jit(solution)/shard_map/ppermute | solution.py:259
  35.7 1.6 %collective-permute-done.5.two = f32[72,128]{1,0:T(8,128)S(1)} collective-permute-done((f32[72,128]{1,0:T(8,128)}, f32[72,128]{1,0:T(8,128)S(1)}, u32[]{:S(2)}, u32[]{:S(2)}) %collective-permute-start.5) | collective-permute-done | bytes 36896 | tf_op jit(solution)/shard_map/ppermute | solution.py:259
  37.3 0.7 %collective-permute-done.6.three = f32[72,128]{1,0:T(8,128)S(1)} collective-permute-done((f32[72,128]{1,0:T(8,128)}, f32[72,128]{1,0:T(8,128)S(1)}, u32[]{:S(2)}, u32[]{:S(2)}) %collective-permute-start.6) | collective-permute-done | bytes 36896 | tf_op jit(solution)/shard_map/ppermute | solution.py:259
  38.0 0.0 copy-done.3
  38.0 0.6 %copy-done.5 = f32[72,128]{1,0:T(8,128)} copy-done((f32[72,128]{1,0:T(8,128)}, f32[72,128]{1,0:T(8,128)S(1)}, u32[]{:S(2)}) %copy-start.5) | copy-done | bytes 36888
  38.6 1.7 %tension.2 = (f32[8,2,128]{2,1,0:T(2,128)}, f32[8,2,128]{2,1,0:T(2,128)}) custom-call(f32[72,128]{1,0:T(8,128)} %get-tuple-element.18.own, f32[72,128]{1,0:T(8,128)} %copy-done.3, f32[72,128]{1,0:T(8,128)} %copy-done.4, f32[72,128]{1,0:T(8,128)} %copy-done.5, f32[8,2,128]{2,1,0:T(2,128)} %troponin.1, f32[8,2,128]{2,1,0:T(2,128)} %tension.3, ...), custom_call_target="tpu_custom_call" | custom-call | tf_op jit(solution)/shard_map/tension/pallas_call | solution.py:334
  (8 shorter events, 0.0 us)
Async XLA Ops:
  9.5 8.4 %collective-permute-start = (f32[48,128]{1,0:T(8,128)}, f32[48,128]{1,0:T(8,128)S(1)}, u32[]{:S(2)}, u32[]{:S(2)}) collective-permute-start(f32[48,128]{1,0:T(8,128)} %get-tuple-element.13), channel_id=1, source_target_pairs={{0,16},{16,32},{32,48},{48,64},{64,80},{80,96},{96,112},{1,17},{17... | collective-permute-start | bytes 73736 | tf_op jit(solution)/shard_map/ppermute | solution.py:319
  17.9 0.6 %copy-start.6 = (f32[48,128]{1,0:T(8,128)}, f32[48,128]{1,0:T(8,128)S(1)}, u32[]{:S(2)}) copy-start(f32[48,128]{1,0:T(8,128)S(1)} %collective-permute-done.incoming) | copy-start | bytes 73732
  20.2 5.0 %collective-permute-start.1 = (f32[104,128]{1,0:T(8,128)}, f32[104,128]{1,0:T(8,128)S(1)}, u32[]{:S(2)}, u32[]{:S(2)}) collective-permute-start(f32[104,128]{1,0:T(8,128)} %get-tuple-element.15), channel_id=1, source_target_pairs={{0,1},{1,2},{2,3},{3,0},{4,5},{5,6},{6,7},{7,4},{8,9},{9,10},{10,1... | collective-permute-start | bytes 159752 | tf_op jit(solution)/shard_map/ppermute | solution.py:259
  21.5 4.9 %collective-permute-start.2 = (f32[104,128]{1,0:T(8,128)}, f32[104,128]{1,0:T(8,128)S(1)}, u32[]{:S(2)}, u32[]{:S(2)}) collective-permute-start(f32[104,128]{1,0:T(8,128)} %get-tuple-element.16), channel_id=1, source_target_pairs={{0,2},{1,3},{2,0},{3,1},{4,6},{5,7},{6,4},{7,5},{8,10},{9,11},{10,... | collective-permute-start | bytes 159752 | tf_op jit(solution)/shard_map/ppermute | solution.py:259
  24.1 3.3 %collective-permute-start.3 = (f32[104,128]{1,0:T(8,128)}, f32[104,128]{1,0:T(8,128)S(1)}, u32[]{:S(2)}, u32[]{:S(2)}) collective-permute-start(f32[104,128]{1,0:T(8,128)} %get-tuple-element.17), channel_id=1, source_target_pairs={{0,3},{1,0},{2,1},{3,2},{4,7},{5,4},{6,5},{7,6},{8,11},{9,8},{10,9... | collective-permute-start | bytes 159752 | tf_op jit(solution)/shard_map/ppermute | solution.py:259
  25.1 2.2 %copy-start = (f32[104,128]{1,0:T(8,128)}, f32[104,128]{1,0:T(8,128)S(1)}, u32[]{:S(2)}) copy-start(f32[104,128]{1,0:T(8,128)S(1)} %collective-permute-done.1.one) | copy-start | bytes 159748
  26.4 1.0 %copy-start.1 = (f32[104,128]{1,0:T(8,128)}, f32[104,128]{1,0:T(8,128)S(1)}, u32[]{:S(2)}) copy-start(f32[104,128]{1,0:T(8,128)S(1)} %collective-permute-done.2.two) | copy-start | bytes 159748
  27.4 0.6 %copy-start.2 = (f32[104,128]{1,0:T(8,128)}, f32[104,128]{1,0:T(8,128)S(1)}, u32[]{:S(2)}) copy-start(f32[104,128]{1,0:T(8,128)S(1)} %collective-permute-done.3.three) | copy-start | bytes 159748
  29.7 6.0 %collective-permute-start.4 = (f32[72,128]{1,0:T(8,128)}, f32[72,128]{1,0:T(8,128)S(1)}, u32[]{:S(2)}, u32[]{:S(2)}) collective-permute-start(f32[72,128]{1,0:T(8,128)} %get-tuple-element.19), channel_id=1, source_target_pairs={{0,4},{4,8},{8,12},{12,0},{1,5},{5,9},{9,13},{13,1},{2,6},{6,10},{... | collective-permute-start | bytes 110600 | tf_op jit(solution)/shard_map/ppermute | solution.py:259
  34.3 3.0 %collective-permute-start.5 = (f32[72,128]{1,0:T(8,128)}, f32[72,128]{1,0:T(8,128)S(1)}, u32[]{:S(2)}, u32[]{:S(2)}) collective-permute-start(f32[72,128]{1,0:T(8,128)} %get-tuple-element.20), channel_id=1, source_target_pairs={{0,8},{4,12},{8,0},{12,4},{1,9},{5,13},{9,1},{13,5},{2,10},{6,14},... | collective-permute-start | bytes 110600 | tf_op jit(solution)/shard_map/ppermute | solution.py:259
  34.4 3.6 %collective-permute-start.6 = (f32[72,128]{1,0:T(8,128)}, f32[72,128]{1,0:T(8,128)S(1)}, u32[]{:S(2)}, u32[]{:S(2)}) collective-permute-start(f32[72,128]{1,0:T(8,128)} %get-tuple-element.21), channel_id=1, source_target_pairs={{0,12},{4,0},{8,4},{12,8},{1,13},{5,1},{9,5},{13,9},{2,14},{6,2},{... | collective-permute-start | bytes 110600 | tf_op jit(solution)/shard_map/ppermute | solution.py:259
  35.7 2.4 %copy-start.3 = (f32[72,128]{1,0:T(8,128)}, f32[72,128]{1,0:T(8,128)S(1)}, u32[]{:S(2)}) copy-start(f32[72,128]{1,0:T(8,128)S(1)} %collective-permute-done.4.one) | copy-start | bytes 110596
  37.3 0.7 %copy-start.4 = (f32[72,128]{1,0:T(8,128)}, f32[72,128]{1,0:T(8,128)S(1)}, u32[]{:S(2)}) copy-start(f32[72,128]{1,0:T(8,128)S(1)} %collective-permute-done.5.two) | copy-start | bytes 110596
  38.0 0.6 %copy-start.5 = (f32[72,128]{1,0:T(8,128)}, f32[72,128]{1,0:T(8,128)S(1)}, u32[]{:S(2)}) copy-start(f32[72,128]{1,0:T(8,128)S(1)} %collective-permute-done.6.three) | copy-start | bytes 110596
